TPU v7x, 32 devices: a whole 2x2x4 slice. The times are simulated.
32 devices in a mesh: depth: 4 (over z), col: 2 (over y), row: 4 (over x, core).
Axes of the slice: x: 2, y: 2, z: 4, core: 2. Of those that a mesh axis runs over, the one named last changes fastest.
Arguments:
- weight: bfloat16 [3072, 3072], P(('row', 'depth'), 'col')
- rhs_stack: bfloat16 [3, 3072, 8192], P(None, ('row', 'depth'), 'col')
Outputs:
- output: bfloat16 [3, 3072, 8192], P(None, ('row', 'depth'), 'col')
All inputs are finite; a program needn't handle non-finite values.
Results may differ from a plain program's by a relative error of at most 0.001.
Values are sent between devices in bfloat16 or wider.
A program may use at most 1 GiB of HBM per device.

v0:
```python
import functools

import jax
import jax.numpy as jnp
from jax import lax
from jax.experimental import pallas as pl
from jax.experimental.pallas import tpu as pltpu
from jax.sharding import PartitionSpec as P

MESH = pl.DeviceIdType.MESH
WIDTH = 256
AHEAD = 3
LAG = 4


def kernel(width, x_ref, a_ref, o_ref, xb, ab, yb, xa_send, xa_recv, xl_sem, xz_send, xz_recv, xt_recv, a_send, a_recv, al_sem, y_send, y_recv, yl_sem):
    z = lax.axis_index("depth")
    j = lax.axis_index("col")
    i = lax.axis_index("row")
    rhs, rows, cols = x_ref.shape
    quarter = cols // 4
    subs = quarter // width
    chunks = rhs * subs
    half = a_ref.shape[1]
    is_mid = (z + 1) // 2 == 1
    end = (z // 2) * 3
    near = 1 + z // 2
    peer = 3 - z
    core_i = i + 1 - 2 * (i % 2)
    x_i = (i + 2) % 4
    other_i = (core_i + 2) % 4

    def span(owner, sub):
        return pl.ds(pl.multiple_of(owner * quarter + sub * width, width), width)

    def a_unit(e, row, col):
        return ab.at[e, row, :, pl.ds(pl.multiple_of(col * half, half), half)]

    def remote(src, dst, send, recv, where):
        return pltpu.make_async_remote_copy(src_ref=src, dst_ref=dst, send_sem=send, recv_sem=recv, device_id=where, device_id_type=MESH)

    def wait_bytes(ref, sem):
        pltpu.make_async_copy(ref, ref, sem).wait()

    def swap_start(c):
        r, sub = c // subs, c % subs
        for to in (core_i, x_i, other_i):
            remote(x_ref.at[r, :, span(to, sub)], xb.at[c, i, z], xa_send, xa_recv.at[c, i], (z, j, to)).start()

    def own_start(c, to):
        r, sub = c // subs, c % subs
        remote(x_ref.at[r, :, span(i, sub)], xb.at[c, i, z], xz_send, xz_recv.at[c, z], (to, j, i)).start()

    def pass_on(c, to):
        for t in (core_i, x_i, other_i):
            wait_bytes(xb.at[c, t, z], xa_recv.at[c, t])
            remote(xb.at[c, t, z], xb.at[c, t, z], xz_send, xz_recv.at[c, z], (to, j, i)).start()

    def hop_start(c, layer, to):
        remote(xb.at[c, :, layer], xb.at[c, :, layer], xz_send, xz_recv.at[c, layer], (to, j, i)).start()

    def tails(h):
        return xb.at[chunks - 1, :, end, :, pl.ds(h * (width // 2), width // 2)]

    def hop_wait(c, layer):
        wait_bytes(xb.at[c, :, layer], xz_recv.at[c, layer])

    def a_start(src, e, row, col, where):
        remote(src, a_unit(e, row, col), a_send, a_recv.at[e, row, col], where).start()

    def a_wait(e, row, col):
        wait_bytes(a_unit(e, row, col), a_recv.at[e, row, col])

    barrier = pltpu.get_barrier_semaphore()
    for d in (1, 2, 3):
        pl.semaphore_signal(barrier, inc=1, device_id=(z, j, (i + d) % 4), device_id_type=MESH)

    @pl.when(is_mid)
    def _():
        pl.semaphore_signal(barrier, inc=1, device_id=(z, 1 - j, i), device_id_type=MESH)
        pl.semaphore_signal(barrier, inc=1, device_id=(peer, j, i), device_id_type=MESH)
        for t in range(4):
            pl.semaphore_signal(barrier, inc=1, device_id=(end, j, t), device_id_type=MESH)
        pl.semaphore_wait(barrier, 9)

    @pl.when(jnp.logical_not(is_mid))
    def _():
        for t in range(4):
            pl.semaphore_signal(barrier, inc=1, device_id=(near, j, t), device_id_type=MESH)
        pl.semaphore_wait(barrier, 7)

    @pl.when(jnp.logical_not(is_mid))
    def _():
        swap_start(0)
        a_start(a_ref, 0, i, j, (near, j, i))
        own_start(0, near)

        def issue(c, _):
            swap_start(c)
            own_start(c, near)
            return 0

        lax.fori_loop(1, AHEAD, issue, 0)

        def step(c, _):
            @pl.when(c + AHEAD < chunks)
            def _():
                issue(c + AHEAD, 0)

            pass_on(c, near)
            return 0

        lax.fori_loop(0, chunks, step, 0)
        wait_bytes(x_ref.at[:, :, pl.ds(0, 3 * quarter)], xa_send)
        wait_bytes(a_ref, a_send)
        wait_bytes(xb.at[:, :, 0], xz_send)
        wait_bytes(o_ref, y_recv)

    @pl.when(is_mid)
    def _():
        def a_fan(src, e, row):
            a_start(src, e, row, j, (z, 1 - j, i))
            a_start(src, e, row, j, (z, j, core_i))

        def issue(c, _):
            swap_start(c)
            own_start(c, peer)
            return 0

        issue(0, 0)
        a_fan(a_ref, 1, i)
        lax.fori_loop(1, AHEAD, issue, 0)
        a_start(a_ref, 1, i, j, (z, j, x_i))
        pltpu.make_async_copy(a_ref, a_unit(1, i, j), al_sem).start()

        def keep(c, _):
            pltpu.make_async_copy(x_ref.at[c // subs, :, span(i, c % subs)], xb.at[c, i, z], xl_sem).start()
            return 0

        lax.fori_loop(0, chunks, keep, 0)

        def forward(c, _):
            @pl.when(c + AHEAD < chunks)
            def _():
                issue(c + AHEAD, 0)

            pass_on(c, peer)
            return 0

        lax.fori_loop(0, AHEAD, forward, 0)

        def compute(c, at, size):
            r, sub = c // subs, c % subs
            cut = pl.ds(at, size)
            out = pl.ds(pl.multiple_of(i * quarter + sub * width + at, size), size)

            def unit(u, _):
                e, t = u // 4, u % 4
                block = xb[c, :, :, :, cut].reshape(16 * rows, size)
                yb[c, e, t, :, cut] = jnp.dot(ab[e, t], block, preferred_element_type=jnp.float32).astype(yb.dtype)
                layer = end + e * (z - end)
                mine = (e == 1) & (t == i)

                @pl.when(mine)
                def _():
                    pltpu.make_async_copy(yb.at[c, e, t, :, cut], o_ref.at[r, :, out], yl_sem).start()

                @pl.when(jnp.logical_not(mine))
                def _():
                    remote(yb.at[c, e, t, :, cut], o_ref.at[r, :, out], y_send, y_recv, (layer, j, t)).start()

                return 0

            lax.fori_loop(0, 8, unit, 0)

        def step(s, _):
            @pl.when(s < chunks)
            def _():
                hop_wait(s, end)

            @pl.when(s < chunks - 1)
            def _():
                hop_start(s, end, peer)

            @pl.when(s == chunks - 1)
            def _():
                for h in range(2):
                    remote(tails(h), tails(h), xz_send, xt_recv.at[h], (peer, j, i)).start()

            @pl.when(s + AHEAD < chunks)
            def _():
                forward(s + AHEAD, 0)

            @pl.when(s == 0)
            def _():
                a_wait(0, i, j)
                a_fan(a_unit(0, i, j), 0, i)
                a_start(a_unit(0, i, j), 0, i, j, (z, j, x_i))
                a_wait(1, x_i, j)
                a_fan(a_unit(1, x_i, j), 1, x_i)

            @pl.when(s == 1)
            def _():
                a_wait(1, i, 1 - j)
                a_start(a_unit(1, i, 1 - j), 1, i, 1 - j, (z, j, core_i))

            @pl.when(s == 2)
            def _():
                a_wait(0, x_i, j)
                a_fan(a_unit(0, x_i, j), 0, x_i)
                a_wait(0, i, 1 - j)
                a_start(a_unit(0, i, 1 - j), 0, i, 1 - j, (z, j, core_i))

            @pl.when(s == LAG - 1)
            def _():
                for e in (1, 0):
                    a_wait(e, x_i, 1 - j)
                    a_start(a_unit(e, x_i, 1 - j), e, x_i, 1 - j, (z, j, core_i))
                wait_bytes(a_unit(1, i, j), al_sem)
                wait_bytes(xb.at[:, 0, 0], xl_sem)
                for e in (1, 0):
                    for row in (core_i, other_i):
                        for col in range(2):
                            a_wait(e, row, col)

            @pl.when(s >= LAG)
            def _():
                hop_wait(s - LAG, peer)
                hop_wait(s - LAG, 3 - end)
                compute(s - LAG, 0, width)

            return 0

        lax.fori_loop(0, chunks + LAG - 1, step, 0)
        hop_wait(chunks - 1, peer)
        for h in range(2):
            wait_bytes(tails(h), xt_recv.at[h])
            compute(chunks - 1, h * (width // 2), width // 2)
        wait_bytes(x_ref.at[:, :, pl.ds(0, 3 * quarter)], xa_send)
        wait_bytes(ab.at[:, pl.ds(0, 3)], a_send)
        wait_bytes(ab.at[0, 0], a_send)
        wait_bytes(xb.at[:, :, pl.ds(0, 2)], xz_send)
        wait_bytes(yb.at[:, 0], y_send)
        wait_bytes(yb.at[:, 1, pl.ds(0, 3)], y_send)
        wait_bytes(yb.at[:, 1, 0], yl_sem)
        wait_bytes(o_ref.at[:, :, pl.ds(0, 3 * quarter)], y_recv)


def solution(mesh):
    def local_product(a, x):
        rhs, rows, cols = x.shape
        width = WIDTH
        while (cols // 4) % width:
            width //= 2
        chunks = rhs * (cols // 4 // width)
        dma = pltpu.SemaphoreType.DMA
        return pl.pallas_call(
            functools.partial(kernel, width),
            out_shape=pltpu.VMEM(x.shape, x.dtype),
            in_specs=[pl.BlockSpec(memory_space=pltpu.HBM)] * 2,
            out_specs=pl.BlockSpec(memory_space=pltpu.VMEM),
            scratch_shapes=[
                pltpu.VMEM((chunks, 4, 4, rows, width), x.dtype),
                pltpu.VMEM((2, 4, rows, 2 * a.shape[1]), a.dtype),
                pltpu.VMEM((chunks, 2, 4, rows, width), x.dtype),
                dma, dma((chunks, 4)), dma,
                dma, dma((chunks, 4)), dma((2,)),
                dma, dma((2, 4, 2)), dma,
                dma, dma, dma,
            ],
            compiler_params=pltpu.CompilerParams(collective_id=0, has_side_effects=True, vmem_limit_bytes=int(56.5 * 2**20)),
        )(x, a)

    return jax.shard_map(local_product, mesh=mesh, in_specs=(P(("row", "depth"), "col"), P(None, ("row", "depth"), "col")), out_specs=P(None, ("row", "depth"), "col"), check_vma=False)
```

profile of v0, /device:TPU:0, one launch (start us, length us, event | category | flops | bytes accessed | tf_op | source)
XLA Modules:
  0.0 221.5 jit_solution(11761912169117927075)
XLA Ops:
  0.0 219.3 %shard_map.28 = bf16[3,192,4096]{2,1,0:T(8,128)(2,1)S(1)} custom-call(bf16[3,192,4096]{2,1,0:T(8,128)(2,1)} %x_ref.1, bf16[192,1536]{1,0:T(8,128)(2,1)} %a_ref.1), custom_call_target="tpu_custom_call" | custom-call | tf_op jit(solution)/shard_map/pallas_call | solution.py:257
  219.3 2.2 copy.4
where the time goes:
time: 222 us
  Pallas kernels  219 us (99%)
    pallas_call x1, Pallas kernels, local_product(): pl.pallas_call(functools.partial(kernel, width), out_shape=pltpu.VMEM(x.s...  219 us

commit v1 on v0

--- a/solution.py
+++ b/solution.py
@@ -13,7 +13,7 @@
 LAG = 4
 
 
-def kernel(width, x_ref, a_ref, o_ref, xb, ab, yb, xa_send, xa_recv, xl_sem, xz_send, xz_recv, xt_recv, a_send, a_recv, al_sem, y_send, y_recv, yl_sem):
+def kernel(width, x_ref, a_ref, o_ref, xb, ab, yb, xa_send, xa_recv, xl_sem, xz_send, xz_recv, xt_recv, a_send, a_recv, al_sem, y_send, y_recv, yl_sem, ready):
     z = lax.axis_index("depth")
     j = lax.axis_index("col")
     i = lax.axis_index("row")
@@ -81,12 +81,10 @@
         pl.semaphore_signal(barrier, inc=1, device_id=(peer, j, i), device_id_type=MESH)
         for t in range(4):
             pl.semaphore_signal(barrier, inc=1, device_id=(end, j, t), device_id_type=MESH)
-        pl.semaphore_wait(barrier, 9)
+        pl.semaphore_wait(barrier, 5)
 
     @pl.when(jnp.logical_not(is_mid))
     def _():
-        for t in range(4):
-            pl.semaphore_signal(barrier, inc=1, device_id=(near, j, t), device_id_type=MESH)
         pl.semaphore_wait(barrier, 7)
 
     @pl.when(jnp.logical_not(is_mid))
@@ -94,6 +92,8 @@
         swap_start(0)
         a_start(a_ref, 0, i, j, (near, j, i))
         own_start(0, near)
+        for t in range(4):
+            pl.semaphore_signal(ready, inc=1, device_id=(near, j, t), device_id_type=MESH)
 
         def issue(c, _):
             swap_start(c)
@@ -187,9 +187,13 @@
                 for h in range(2):
                     remote(tails(h), tails(h), xz_send, xt_recv.at[h], (peer, j, i)).start()
 
-            @pl.when(s + AHEAD < chunks)
-            def _():
-                forward(s + AHEAD, 0)
+            @pl.when(s == 0)
+            def _():
+                forward(AHEAD, 0)
+
+            @pl.when((s >= AHEAD) & (s + 1 < chunks))
+            def _():
+                forward(s + 1, 0)
 
             @pl.when(s == 0)
             def _():
@@ -217,6 +221,7 @@
                     a_wait(e, x_i, 1 - j)
                     a_start(a_unit(e, x_i, 1 - j), e, x_i, 1 - j, (z, j, core_i))
                 wait_bytes(a_unit(1, i, j), al_sem)
+                pl.semaphore_wait(ready, 4)
                 wait_bytes(xb.at[:, 0, 0], xl_sem)
                 for e in (1, 0):
                     for row in (core_i, other_i):
@@ -266,7 +271,7 @@
                 dma, dma((chunks, 4)), dma,
                 dma, dma((chunks, 4)), dma((2,)),
                 dma, dma((2, 4, 2)), dma,
-                dma, dma, dma,
+                dma, dma, dma, pltpu.SemaphoreType.REGULAR,
             ],
             compiler_params=pltpu.CompilerParams(collective_id=0, has_side_effects=True, vmem_limit_bytes=int(56.5 * 2**20)),
         )(x, a)

time: 222 us -> 217 us (0.977)
  Pallas kernels: 219 us -> 215 us
    pallas_call x1, Pallas kernels: 219 us -> 215 us  [local_product(): pl.pallas_call(functools.partial(kernel, width), out_shape=pltpu.VMEM(x.s...]
where the time goes in v1:
time: 217 us
  Pallas kernels  215 us (99%)
  local copies, waits for them, and re-layouts  2.19 us (1%)
    pallas_call x1, Pallas kernels, local_product(): pl.pallas_call(functools.partial(kernel, width), out_shape=pltpu.VMEM(x.s...  215 us

profile of v1, /device:TPU:0, one launch (start us, length us, event | category | flops | bytes accessed | tf_op | source)
XLA Modules:
  0.0 216.7 jit_solution(157019629323732511)
XLA Ops:
  0.0 214.5 %shard_map.28 = bf16[3,192,4096]{2,1,0:T(8,128)(2,1)S(1)} custom-call(bf16[3,192,4096]{2,1,0:T(8,128)(2,1)} %x_ref.1, bf16[192,1536]{1,0:T(8,128)(2,1)} %a_ref.1), custom_call_target="tpu_custom_call" | custom-call | tf_op jit(solution)/shard_map/pallas_call | solution.py:262
  214.5 2.2 %copy.4 = bf16[3,192,4096]{2,1,0:T(8,128)(2,1)} copy(bf16[3,192,4096]{2,1,0:T(8,128)(2,1)S(1)} %shard_map.28) | data formatting | bytes 9437184

commit v2 on v1

--- a/solution.py
+++ b/solution.py
@@ -13,7 +13,7 @@
 LAG = 4
 
 
-def kernel(width, x_ref, a_ref, o_ref, xb, ab, yb, xa_send, xa_recv, xl_sem, xz_send, xz_recv, xt_recv, a_send, a_recv, al_sem, y_send, y_recv, yl_sem, ready):
+def kernel(width, x_ref, a_ref, o_ref, xb, ab, yb, acc, xa_send, xa_recv, xl_sem, xz_send, xz_recv, xt_recv, a_send, a_recv, al_sem, y_send, y_recv, yl_sem, ready_core, ready_x, ready_y, ready):
     z = lax.axis_index("depth")
     j = lax.axis_index("col")
     i = lax.axis_index("row")
@@ -59,8 +59,21 @@
     def hop_start(c, layer, to):
         remote(xb.at[c, :, layer], xb.at[c, :, layer], xz_send, xz_recv.at[c, layer], (to, j, i)).start()
 
-    def tails(h):
-        return xb.at[chunks - 1, :, end, :, pl.ds(h * (width // 2), width // 2)]
+    last, narrow = chunks - 1, width // 2
+
+    def tail_part(n):
+        if n == 0:
+            return xb.at[last, :, end, :, pl.ds(0, narrow)]
+        return xb.at[last, n - 1, end, :, pl.ds(narrow, narrow)]
+
+    def tail_start(h):
+        for t in (core_i, x_i, other_i):
+            if h == 0:
+                wait_bytes(xb.at[last, t, z], xa_recv.at[last, t])
+            part = xb.at[last, t, z, :, pl.ds(h * narrow, narrow)]
+            remote(part, part, xz_send, xt_recv.at[5 + h], (peer, j, i)).start()
+        for n in (range(1, 5) if h else range(1)):
+            remote(tail_part(n), tail_part(n), xz_send, xt_recv.at[n], (peer, j, i)).start()
 
     def hop_wait(c, layer):
         wait_bytes(xb.at[c, :, layer], xz_recv.at[c, layer])
@@ -71,20 +84,34 @@
     def a_wait(e, row, col):
         wait_bytes(a_unit(e, row, col), a_recv.at[e, row, col])
 
+    def notify(sem, where):
+        pl.semaphore_signal(sem, inc=1, device_id=where, device_id_type=MESH)
+
     barrier = pltpu.get_barrier_semaphore()
-    for d in (1, 2, 3):
-        pl.semaphore_signal(barrier, inc=1, device_id=(z, j, (i + d) % 4), device_id_type=MESH)
 
     @pl.when(is_mid)
     def _():
-        pl.semaphore_signal(barrier, inc=1, device_id=(z, 1 - j, i), device_id_type=MESH)
-        pl.semaphore_signal(barrier, inc=1, device_id=(peer, j, i), device_id_type=MESH)
-        for t in range(4):
-            pl.semaphore_signal(barrier, inc=1, device_id=(end, j, t), device_id_type=MESH)
-        pl.semaphore_wait(barrier, 5)
+        notify(barrier, (peer, j, i))
+
+        @pl.when(i % 2 == 0)
+        def _():
+            notify(barrier, (z, j, core_i))
+
+        @pl.when(i < 2)
+        def _():
+            for to in (x_i, other_i):
+                notify(barrier, (z, j, to))
+
+        @pl.when(j == 0)
+        def _():
+            notify(barrier, (z, 1, i))
+
+        pl.semaphore_wait(barrier, 1 + i % 2 + i // 2 * 2 + j)
 
     @pl.when(jnp.logical_not(is_mid))
     def _():
+        for d in (1, 2, 3):
+            notify(barrier, (z, j, (i + d) % 4))
         pl.semaphore_wait(barrier, 7)
 
     @pl.when(jnp.logical_not(is_mid))
@@ -93,7 +120,7 @@
         a_start(a_ref, 0, i, j, (near, j, i))
         own_start(0, near)
         for t in range(4):
-            pl.semaphore_signal(ready, inc=1, device_id=(near, j, t), device_id_type=MESH)
+            notify(ready, (near, j, t))
 
         def issue(c, _):
             swap_start(c)
@@ -127,9 +154,47 @@
             own_start(c, peer)
             return 0
 
-        issue(0, 0)
+        def first(c, _):
+            own_start(c, peer)
+            return 0
+
+        def swap_more(c, _):
+            swap_start(c)
+            return 0
+
+        lax.fori_loop(0, AHEAD, first, 0)
+        for t in range(4):
+            notify(barrier, (end, j, t))
+
+        @pl.when(i % 2 == 1)
+        def _():
+            notify(ready_core, (z, j, core_i))
+
+        @pl.when(i >= 2)
+        def _():
+            for to in (x_i, other_i):
+                notify(ready_x, (z, j, to))
+
+        @pl.when(j == 1)
+        def _():
+            notify(ready_y, (z, 0, i))
+
+        @pl.when(i % 2 == 0)
+        def _():
+            pl.semaphore_wait(ready_core, 1)
+
+        @pl.when(i < 2)
+        def _():
+            pl.semaphore_wait(ready_x, 2)
+
+        swap_start(0)
+
+        @pl.when(j == 0)
+        def _():
+            pl.semaphore_wait(ready_y, 1)
+
         a_fan(a_ref, 1, i)
-        lax.fori_loop(1, AHEAD, issue, 0)
+        lax.fori_loop(1, AHEAD, swap_more, 0)
         a_start(a_ref, 1, i, j, (z, j, x_i))
         pltpu.make_async_copy(a_ref, a_unit(1, i, j), al_sem).start()
 
@@ -149,15 +214,18 @@
 
         lax.fori_loop(0, AHEAD, forward, 0)
 
-        def compute(c, at, size):
+        def compute(c, at, size, lo=0, hi=8, done=0):
             r, sub = c // subs, c % subs
             cut = pl.ds(at, size)
             out = pl.ds(pl.multiple_of(i * quarter + sub * width + at, size), size)
 
             def unit(u, _):
                 e, t = u // 4, u % 4
-                block = xb[c, :, :, :, cut].reshape(16 * rows, size)
-                yb[c, e, t, :, cut] = jnp.dot(ab[e, t], block, preferred_element_type=jnp.float32).astype(yb.dtype)
+                block = xb[c, done:, :, :, cut].reshape((4 - done) * 4 * rows, size)
+                total = jnp.dot(ab[e, t, :, done * 4 * rows :], block, preferred_element_type=jnp.float32)
+                if done:
+                    total = total + acc[t]
+                yb[c, e, t, :, cut] = total.astype(yb.dtype)
                 layer = end + e * (z - end)
                 mine = (e == 1) & (t == i)
 
@@ -171,7 +239,7 @@
 
                 return 0
 
-            lax.fori_loop(0, 8, unit, 0)
+            lax.fori_loop(lo, hi, unit, 0)
 
         def step(s, _):
             @pl.when(s < chunks)
@@ -182,16 +250,19 @@
             def _():
                 hop_start(s, end, peer)
 
-            @pl.when(s == chunks - 1)
-            def _():
-                for h in range(2):
-                    remote(tails(h), tails(h), xz_send, xt_recv.at[h], (peer, j, i)).start()
+            @pl.when(s == last)
+            def _():
+                tail_start(0)
+
+            @pl.when((s == last) & (i % 2 == 0))
+            def _():
+                tail_start(1)
 
             @pl.when(s == 0)
             def _():
                 forward(AHEAD, 0)
 
-            @pl.when((s >= AHEAD) & (s + 1 < chunks))
+            @pl.when((s >= AHEAD) & (s + 1 < last))
             def _():
                 forward(s + 1, 0)
 
@@ -237,10 +308,26 @@
             return 0
 
         lax.fori_loop(0, chunks + LAG - 1, step, 0)
-        hop_wait(chunks - 1, peer)
-        for h in range(2):
-            wait_bytes(tails(h), xt_recv.at[h])
-            compute(chunks - 1, h * (width // 2), width // 2)
+        wait_bytes(xb.at[last, 0, peer], xz_recv.at[last, peer])
+        wait_bytes(xb.at[last, pl.ds(0, 3), peer, :, pl.ds(0, narrow)], xt_recv.at[5])
+        wait_bytes(tail_part(0), xt_recv.at[0])
+        compute(last, 0, narrow, 0, 4)
+
+        @pl.when(i % 2 == 1)
+        def _():
+            tail_start(1)
+
+        compute(last, 0, narrow, 4, 8)
+        wait_bytes(xb.at[last, pl.ds(0, 3), peer, :, pl.ds(0, narrow)], xt_recv.at[6])
+        for n in range(3):
+            wait_bytes(tail_part(n + 1), xt_recv.at[n + 1])
+            rhs_part = xb[last, n, :, :, pl.ds(narrow, narrow)].reshape(4 * rows, narrow)
+            lhs_part = ab[0, :, :, 4 * rows * n : 4 * rows * (n + 1)].reshape(4 * rows, 4 * rows)
+            sums = jnp.dot(lhs_part, rhs_part, preferred_element_type=jnp.float32).reshape(4, rows, narrow)
+            acc[...] = sums if n == 0 else acc[...] + sums
+        wait_bytes(tail_part(4), xt_recv.at[4])
+        compute(last, narrow, narrow, 0, 4, 3)
+        compute(last, narrow, narrow, 4, 8)
         wait_bytes(x_ref.at[:, :, pl.ds(0, 3 * quarter)], xa_send)
         wait_bytes(ab.at[:, pl.ds(0, 3)], a_send)
         wait_bytes(ab.at[0, 0], a_send)
@@ -268,10 +355,11 @@
                 pltpu.VMEM((chunks, 4, 4, rows, width), x.dtype),
                 pltpu.VMEM((2, 4, rows, 2 * a.shape[1]), a.dtype),
                 pltpu.VMEM((chunks, 2, 4, rows, width), x.dtype),
+                pltpu.VMEM((4, rows, width // 2), jnp.float32),
                 dma, dma((chunks, 4)), dma,
-                dma, dma((chunks, 4)), dma((2,)),
+                dma, dma((chunks, 4)), dma((7,)),
                 dma, dma((2, 4, 2)), dma,
-                dma, dma, dma, pltpu.SemaphoreType.REGULAR,
+                dma, dma, dma, pltpu.SemaphoreType.REGULAR, pltpu.SemaphoreType.REGULAR, pltpu.SemaphoreType.REGULAR, pltpu.SemaphoreType.REGULAR,
             ],
             compiler_params=pltpu.CompilerParams(collective_id=0, has_side_effects=True, vmem_limit_bytes=int(56.5 * 2**20)),
         )(x, a)

time: 217 us -> 215 us (level)
  no operation moved by 1% of the time
where the time goes in v2:
time: 215 us
  Pallas kernels  213 us (99%)
  local copies, waits for them, and re-layouts  2.19 us (1%)
    pallas_call x1, Pallas kernels, local_product(): pl.pallas_call(functools.partial(kernel, width), out_shape=pltpu.VMEM(x.s...  213 us

profile of v2, /device:TPU:0, one launch (start us, length us, event | category | flops | bytes accessed | tf_op | source)
XLA Modules:
  0.0 215.2 jit_solution(7456733492260657433)
XLA Ops:
  0.0 213.0 %shard_map.28 = bf16[3,192,4096]{2,1,0:T(8,128)(2,1)S(1)} custom-call(bf16[3,192,4096]{2,1,0:T(8,128)(2,1)} %x_ref.1, bf16[192,1536]{1,0:T(8,128)(2,1)} %a_ref.1), custom_call_target="tpu_custom_call" | custom-call | tf_op jit(solution)/shard_map/pallas_call | solution.py:349
  213.0 2.2 %copy.4 = bf16[3,192,4096]{2,1,0:T(8,128)(2,1)} copy(bf16[3,192,4096]{2,1,0:T(8,128)(2,1)S(1)} %shard_map.28) | data formatting | bytes 9437184

commit v3 on v2

--- a/solution.py
+++ b/solution.py
@@ -13,7 +13,7 @@
 LAG = 4
 
 
-def kernel(width, x_ref, a_ref, o_ref, xb, ab, yb, acc, xa_send, xa_recv, xl_sem, xz_send, xz_recv, xt_recv, a_send, a_recv, al_sem, y_send, y_recv, yl_sem, ready_core, ready_x, ready_y, ready):
+def kernel(width, x_ref, a_ref, o_ref, xb, ab, yb, acc, xa_send, xa_first, xa_recv, xl_sem, xz_send, xe_recv, xp_recv, xt_recv, a_send, a_end, a_x, a_y, a_core, al_sem, y_send, y_recv, yl_sem, ready_core, ready_x, ready_y, ready):
     z = lax.axis_index("depth")
     j = lax.axis_index("col")
     i = lax.axis_index("row")
@@ -42,47 +42,44 @@
     def wait_bytes(ref, sem):
         pltpu.make_async_copy(ref, ref, sem).wait()
 
+    def first_chunk(c):
+        return isinstance(c, int) and c == 0
+
     def swap_start(c):
         r, sub = c // subs, c % subs
+        arrived = xa_first.at[i] if first_chunk(c) else xa_recv.at[c]
         for to in (core_i, x_i, other_i):
-            remote(x_ref.at[r, :, span(to, sub)], xb.at[c, i, z], xa_send, xa_recv.at[c, i], (z, j, to)).start()
-
-    def own_start(c, to):
+            remote(x_ref.at[r, :, span(to, sub)], xb.at[c, i, z], xa_send, arrived, (z, j, to)).start()
+
+    def own_start(c, to, arrived):
         r, sub = c // subs, c % subs
-        remote(x_ref.at[r, :, span(i, sub)], xb.at[c, i, z], xz_send, xz_recv.at[c, z], (to, j, i)).start()
-
-    def pass_on(c, to):
+        remote(x_ref.at[r, :, span(i, sub)], xb.at[c, i, z], xz_send, arrived.at[c], (to, j, i)).start()
+
+    def pass_on(c, to, arrived):
+        if not first_chunk(c):
+            wait_bytes(xb.at[c, pl.ds(0, 3), z], xa_recv.at[c])
         for t in (core_i, x_i, other_i):
-            wait_bytes(xb.at[c, t, z], xa_recv.at[c, t])
-            remote(xb.at[c, t, z], xb.at[c, t, z], xz_send, xz_recv.at[c, z], (to, j, i)).start()
-
-    def hop_start(c, layer, to):
-        remote(xb.at[c, :, layer], xb.at[c, :, layer], xz_send, xz_recv.at[c, layer], (to, j, i)).start()
+            if first_chunk(c):
+                wait_bytes(xb.at[c, t, z], xa_first.at[t])
+            remote(xb.at[c, t, z], xb.at[c, t, z], xz_send, arrived.at[c], (to, j, i)).start()
 
     last, narrow = chunks - 1, width // 2
 
     def tail_part(n):
         if n == 0:
             return xb.at[last, :, end, :, pl.ds(0, narrow)]
-        return xb.at[last, n - 1, end, :, pl.ds(narrow, narrow)]
+        return xb.at[last, pl.ds(2 * n - 2, 2), end, :, pl.ds(narrow, narrow)]
 
     def tail_start(h):
-        for t in (core_i, x_i, other_i):
-            if h == 0:
-                wait_bytes(xb.at[last, t, z], xa_recv.at[last, t])
-            part = xb.at[last, t, z, :, pl.ds(h * narrow, narrow)]
-            remote(part, part, xz_send, xt_recv.at[5 + h], (peer, j, i)).start()
-        for n in (range(1, 5) if h else range(1)):
+        if h == 0:
+            wait_bytes(xb.at[last, pl.ds(0, 3), z], xa_recv.at[last])
+        part = xb.at[last, :, z, :, pl.ds(h * narrow, narrow)]
+        remote(part, part, xz_send, xt_recv.at[h], (peer, j, i)).start()
+        for n in ((1, 2) if h else (0,)):
             remote(tail_part(n), tail_part(n), xz_send, xt_recv.at[n], (peer, j, i)).start()
 
-    def hop_wait(c, layer):
-        wait_bytes(xb.at[c, :, layer], xz_recv.at[c, layer])
-
-    def a_start(src, e, row, col, where):
-        remote(src, a_unit(e, row, col), a_send, a_recv.at[e, row, col], where).start()
-
-    def a_wait(e, row, col):
-        wait_bytes(a_unit(e, row, col), a_recv.at[e, row, col])
+    def a_start(src, e, row, col, arrived, where):
+        remote(src, a_unit(e, row, col), a_send, arrived, where).start()
 
     def notify(sem, where):
         pl.semaphore_signal(sem, inc=1, device_id=where, device_id_type=MESH)
@@ -117,14 +114,14 @@
     @pl.when(jnp.logical_not(is_mid))
     def _():
         swap_start(0)
-        a_start(a_ref, 0, i, j, (near, j, i))
-        own_start(0, near)
+        a_start(a_ref, 0, i, j, a_end, (near, j, i))
+        own_start(0, near, xe_recv)
         for t in range(4):
             notify(ready, (near, j, t))
 
         def issue(c, _):
             swap_start(c)
-            own_start(c, near)
+            own_start(c, near, xe_recv)
             return 0
 
         lax.fori_loop(1, AHEAD, issue, 0)
@@ -134,10 +131,11 @@
             def _():
                 issue(c + AHEAD, 0)
 
-            pass_on(c, near)
-            return 0
-
-        lax.fori_loop(0, chunks, step, 0)
+            pass_on(c, near, xe_recv)
+            return 0
+
+        step(0, 0)
+        lax.fori_loop(1, chunks, step, 0)
         wait_bytes(x_ref.at[:, :, pl.ds(0, 3 * quarter)], xa_send)
         wait_bytes(a_ref, a_send)
         wait_bytes(xb.at[:, :, 0], xz_send)
@@ -146,16 +144,20 @@
     @pl.when(is_mid)
     def _():
         def a_fan(src, e, row):
-            a_start(src, e, row, j, (z, 1 - j, i))
-            a_start(src, e, row, j, (z, j, core_i))
+            a_start(src, e, row, j, a_y.at[e, 0 if row is i else 1], (z, 1 - j, i))
+            a_start(src, e, row, j, a_core, (z, j, core_i))
 
         def issue(c, _):
             swap_start(c)
-            own_start(c, peer)
+
+            @pl.when(c < last)
+            def _():
+                own_start(c, peer, xp_recv)
+
             return 0
 
         def first(c, _):
-            own_start(c, peer)
+            own_start(c, peer, xp_recv)
             return 0
 
         def swap_more(c, _):
@@ -195,7 +197,7 @@
 
         a_fan(a_ref, 1, i)
         lax.fori_loop(1, AHEAD, swap_more, 0)
-        a_start(a_ref, 1, i, j, (z, j, x_i))
+        a_start(a_ref, 1, i, j, a_x.at[1], (z, j, x_i))
         pltpu.make_async_copy(a_ref, a_unit(1, i, j), al_sem).start()
 
         def keep(c, _):
@@ -209,10 +211,11 @@
             def _():
                 issue(c + AHEAD, 0)
 
-            pass_on(c, peer)
-            return 0
-
-        lax.fori_loop(0, AHEAD, forward, 0)
+            pass_on(c, peer, xp_recv)
+            return 0
+
+        forward(0, 0)
+        lax.fori_loop(1, AHEAD, forward, 0)
 
         def compute(c, at, size, lo=0, hi=8, done=0):
             r, sub = c // subs, c % subs
@@ -244,11 +247,11 @@
         def step(s, _):
             @pl.when(s < chunks)
             def _():
-                hop_wait(s, end)
+                wait_bytes(xb.at[s, :, end], xe_recv.at[s])
 
             @pl.when(s < chunks - 1)
             def _():
-                hop_start(s, end, peer)
+                remote(xb.at[s, :, end], xb.at[s, :, end], xz_send, xp_recv.at[s], (peer, j, i)).start()
 
             @pl.when(s == last)
             def _():
@@ -268,65 +271,58 @@
 
             @pl.when(s == 0)
             def _():
-                a_wait(0, i, j)
+                wait_bytes(a_ref, a_end)
                 a_fan(a_unit(0, i, j), 0, i)
-                a_start(a_unit(0, i, j), 0, i, j, (z, j, x_i))
-                a_wait(1, x_i, j)
+                a_start(a_unit(0, i, j), 0, i, j, a_x.at[0], (z, j, x_i))
+                wait_bytes(a_ref, a_x.at[1])
                 a_fan(a_unit(1, x_i, j), 1, x_i)
 
+            def a_turn(e, k):
+                wait_bytes(a_ref, a_y.at[e, k])
+                row = x_i if k else i
+                a_start(a_unit(e, row, 1 - j), e, row, 1 - j, a_core, (z, j, core_i))
+
             @pl.when(s == 1)
             def _():
-                a_wait(1, i, 1 - j)
-                a_start(a_unit(1, i, 1 - j), 1, i, 1 - j, (z, j, core_i))
+                a_turn(1, 0)
 
             @pl.when(s == 2)
             def _():
-                a_wait(0, x_i, j)
+                wait_bytes(a_ref, a_x.at[0])
                 a_fan(a_unit(0, x_i, j), 0, x_i)
-                a_wait(0, i, 1 - j)
-                a_start(a_unit(0, i, 1 - j), 0, i, 1 - j, (z, j, core_i))
+                a_turn(0, 0)
 
             @pl.when(s == LAG - 1)
             def _():
-                for e in (1, 0):
-                    a_wait(e, x_i, 1 - j)
-                    a_start(a_unit(e, x_i, 1 - j), e, x_i, 1 - j, (z, j, core_i))
+                a_turn(1, 1)
+                a_turn(0, 1)
                 wait_bytes(a_unit(1, i, j), al_sem)
                 pl.semaphore_wait(ready, 4)
                 wait_bytes(xb.at[:, 0, 0], xl_sem)
-                for e in (1, 0):
-                    for row in (core_i, other_i):
-                        for col in range(2):
-                            a_wait(e, row, col)
+                wait_bytes(ab.at[0], a_core)
 
             @pl.when(s >= LAG)
             def _():
-                hop_wait(s - LAG, peer)
-                hop_wait(s - LAG, 3 - end)
+                wait_bytes(xb.at[s - LAG, :, pl.ds(0, 2)], xp_recv.at[s - LAG])
                 compute(s - LAG, 0, width)
 
             return 0
 
         lax.fori_loop(0, chunks + LAG - 1, step, 0)
-        wait_bytes(xb.at[last, 0, peer], xz_recv.at[last, peer])
-        wait_bytes(xb.at[last, pl.ds(0, 3), peer, :, pl.ds(0, narrow)], xt_recv.at[5])
-        wait_bytes(tail_part(0), xt_recv.at[0])
-        compute(last, 0, narrow, 0, 4)
+        wait_bytes(xb.at[pl.ds(0, 8), 0, 0, :, pl.ds(0, narrow)], xt_recv.at[0])
+        compute(last, 0, narrow, 0, 5)
 
         @pl.when(i % 2 == 1)
         def _():
             tail_start(1)
 
-        compute(last, 0, narrow, 4, 8)
-        wait_bytes(xb.at[last, pl.ds(0, 3), peer, :, pl.ds(0, narrow)], xt_recv.at[6])
-        for n in range(3):
-            wait_bytes(tail_part(n + 1), xt_recv.at[n + 1])
-            rhs_part = xb[last, n, :, :, pl.ds(narrow, narrow)].reshape(4 * rows, narrow)
-            lhs_part = ab[0, :, :, 4 * rows * n : 4 * rows * (n + 1)].reshape(4 * rows, 4 * rows)
-            sums = jnp.dot(lhs_part, rhs_part, preferred_element_type=jnp.float32).reshape(4, rows, narrow)
-            acc[...] = sums if n == 0 else acc[...] + sums
-        wait_bytes(tail_part(4), xt_recv.at[4])
-        compute(last, narrow, narrow, 0, 4, 3)
+        compute(last, 0, narrow, 5, 8)
+        wait_bytes(xb.at[pl.ds(0, 6), 0, 0, :, pl.ds(0, narrow)], xt_recv.at[1])
+        rhs_part = xb[last, :2, :, :, pl.ds(narrow, narrow)].reshape(8 * rows, narrow)
+        lhs_part = ab[0, :, :, : 8 * rows].reshape(4 * rows, 8 * rows)
+        acc[...] = jnp.dot(lhs_part, rhs_part, preferred_element_type=jnp.float32).reshape(4, rows, narrow)
+        wait_bytes(tail_part(2), xt_recv.at[2])
+        compute(last, narrow, narrow, 0, 4, 2)
         compute(last, narrow, narrow, 4, 8)
         wait_bytes(x_ref.at[:, :, pl.ds(0, 3 * quarter)], xa_send)
         wait_bytes(ab.at[:, pl.ds(0, 3)], a_send)
@@ -356,9 +352,9 @@
                 pltpu.VMEM((2, 4, rows, 2 * a.shape[1]), a.dtype),
                 pltpu.VMEM((chunks, 2, 4, rows, width), x.dtype),
                 pltpu.VMEM((4, rows, width // 2), jnp.float32),
-                dma, dma((chunks, 4)), dma,
-                dma, dma((chunks, 4)), dma((7,)),
-                dma, dma((2, 4, 2)), dma,
+                dma, dma((4,)), dma((chunks,)), dma,
+                dma, dma((chunks,)), dma((chunks,)), dma((3,)),
+                dma, dma, dma((2,)), dma((2, 2)), dma, dma,
                 dma, dma, dma, pltpu.SemaphoreType.REGULAR, pltpu.SemaphoreType.REGULAR, pltpu.SemaphoreType.REGULAR, pltpu.SemaphoreType.REGULAR,
             ],
             compiler_params=pltpu.CompilerParams(collective_id=0, has_side_effects=True, vmem_limit_bytes=int(56.5 * 2**20)),

time: 215 us -> 214 us (level)
  no operation moved by 1% of the time
where the time goes in v3:
time: 214 us
  Pallas kernels  211 us (99%)
  local copies, waits for them, and re-layouts  2.19 us (1%)
    pallas_call x1, Pallas kernels, local_product(): pl.pallas_call(functools.partial(kernel, width), out_shape=pltpu.VMEM(x.s...  211 us

profile of v3, /device:TPU:0, one launch (start us, length us, event | category | flops | bytes accessed | tf_op | source)
XLA Modules:
  0.0 213.6 jit_solution(5512652121930963921)
XLA Ops:
  0.0 211.4 %shard_map.28 = bf16[3,192,4096]{2,1,0:T(8,128)(2,1)S(1)} custom-call(bf16[3,192,4096]{2,1,0:T(8,128)(2,1)} %x_ref.1, bf16[192,1536]{1,0:T(8,128)(2,1)} %a_ref.1), custom_call_target="tpu_custom_call" | custom-call | tf_op jit(solution)/shard_map/pallas_call | solution.py:345
  211.4 2.2 %copy.4 = bf16[3,192,4096]{2,1,0:T(8,128)(2,1)} copy(bf16[3,192,4096]{2,1,0:T(8,128)(2,1)S(1)} %shard_map.28) | data formatting | bytes 9437184

commit v4 on v3

--- a/solution.py
+++ b/solution.py
@@ -13,7 +13,7 @@
 LAG = 4
 
 
-def kernel(width, x_ref, a_ref, o_ref, xb, ab, yb, acc, xa_send, xa_first, xa_recv, xl_sem, xz_send, xe_recv, xp_recv, xt_recv, a_send, a_end, a_x, a_y, a_core, al_sem, y_send, y_recv, yl_sem, ready_core, ready_x, ready_y, ready):
+def kernel(width, x_ref, a_ref, o_ref, xb, ab, yb, acc, sent, xa_first, xa_recv, kept, xe_recv, xp_recv, xt_recv, a_end, a_x, a_y, a_core, y_recv, yl_sem, ready_core, ready_x, ready_y, ready):
     z = lax.axis_index("depth")
     j = lax.axis_index("col")
     i = lax.axis_index("row")
@@ -21,6 +21,7 @@
     quarter = cols // 4
     subs = quarter // width
     chunks = rhs * subs
+    last, narrow = chunks - 1, width // 2
     half = a_ref.shape[1]
     is_mid = (z + 1) // 2 == 1
     end = (z // 2) * 3
@@ -42,28 +43,41 @@
     def wait_bytes(ref, sem):
         pltpu.make_async_copy(ref, ref, sem).wait()
 
-    def first_chunk(c):
-        return isinstance(c, int) and c == 0
+    def early(c):
+        return isinstance(c, int) and c < AHEAD
+
+    def swap_slot(c):
+        return xa_recv.at[c - 1 if early(c) else AHEAD - 1 + (c - AHEAD) // 2]
 
     def swap_start(c):
         r, sub = c // subs, c % subs
-        arrived = xa_first.at[i] if first_chunk(c) else xa_recv.at[c]
+        arrived = xa_first.at[i] if early(c) and c == 0 else swap_slot(c)
         for to in (core_i, x_i, other_i):
-            remote(x_ref.at[r, :, span(to, sub)], xb.at[c, i, z], xa_send, arrived, (z, j, to)).start()
+            remote(x_ref.at[r, :, span(to, sub)], xb.at[c, i, z], sent, arrived, (z, j, to)).start()
 
     def own_start(c, to, arrived):
         r, sub = c // subs, c % subs
-        remote(x_ref.at[r, :, span(i, sub)], xb.at[c, i, z], xz_send, arrived.at[c], (to, j, i)).start()
+        remote(x_ref.at[r, :, span(i, sub)], xb.at[c, i, z], sent, arrived.at[c], (to, j, i)).start()
 
     def pass_on(c, to, arrived):
-        if not first_chunk(c):
-            wait_bytes(xb.at[c, pl.ds(0, 3), z], xa_recv.at[c])
+        if early(c):
+            if c:
+                wait_bytes(xb.at[c, pl.ds(0, 3), z], swap_slot(c))
+        else:
+            opens = (c - AHEAD) % 2 == 0
+
+            @pl.when(jnp.logical_and(opens, c < last))
+            def _():
+                wait_bytes(xb.at[pl.ds(0, 2), pl.ds(0, 3), z], swap_slot(c))
+
+            @pl.when(jnp.logical_and(opens, c == last))
+            def _():
+                wait_bytes(xb.at[c, pl.ds(0, 3), z], swap_slot(c))
+
         for t in (core_i, x_i, other_i):
-            if first_chunk(c):
+            if early(c) and c == 0:
                 wait_bytes(xb.at[c, t, z], xa_first.at[t])
-            remote(xb.at[c, t, z], xb.at[c, t, z], xz_send, arrived.at[c], (to, j, i)).start()
-
-    last, narrow = chunks - 1, width // 2
+            remote(xb.at[c, t, z], xb.at[c, t, z], sent, arrived.at[c], (to, j, i)).start()
 
     def tail_part(n):
         if n == 0:
@@ -72,14 +86,14 @@
 
     def tail_start(h):
         if h == 0:
-            wait_bytes(xb.at[last, pl.ds(0, 3), z], xa_recv.at[last])
+            wait_bytes(xb.at[last, pl.ds(0, 3), z], swap_slot(last))
         part = xb.at[last, :, z, :, pl.ds(h * narrow, narrow)]
-        remote(part, part, xz_send, xt_recv.at[h], (peer, j, i)).start()
+        remote(part, part, sent, xt_recv.at[h], (peer, j, i)).start()
         for n in ((1, 2) if h else (0,)):
-            remote(tail_part(n), tail_part(n), xz_send, xt_recv.at[n], (peer, j, i)).start()
+            remote(tail_part(n), tail_part(n), sent, xt_recv.at[n], (peer, j, i)).start()
 
     def a_start(src, e, row, col, arrived, where):
-        remote(src, a_unit(e, row, col), a_send, arrived, where).start()
+        remote(src, a_unit(e, row, col), sent, arrived, where).start()
 
     def notify(sem, where):
         pl.semaphore_signal(sem, inc=1, device_id=where, device_id_type=MESH)
@@ -124,7 +138,8 @@
             own_start(c, near, xe_recv)
             return 0
 
-        lax.fori_loop(1, AHEAD, issue, 0)
+        for c in range(1, AHEAD):
+            issue(c, 0)
 
         def step(c, _):
             @pl.when(c + AHEAD < chunks)
@@ -134,11 +149,12 @@
             pass_on(c, near, xe_recv)
             return 0
 
-        step(0, 0)
-        lax.fori_loop(1, chunks, step, 0)
-        wait_bytes(x_ref.at[:, :, pl.ds(0, 3 * quarter)], xa_send)
-        wait_bytes(a_ref, a_send)
-        wait_bytes(xb.at[:, :, 0], xz_send)
+        for c in range(AHEAD):
+            step(c, 0)
+        lax.fori_loop(AHEAD, chunks, step, 0)
+        wait_bytes(x_ref.at[:, :, pl.ds(0, 3 * quarter)], sent)
+        wait_bytes(a_ref, sent)
+        wait_bytes(xb.at[:, :, 0], sent)
         wait_bytes(o_ref, y_recv)
 
     @pl.when(is_mid)
@@ -160,10 +176,6 @@
             own_start(c, peer, xp_recv)
             return 0
 
-        def swap_more(c, _):
-            swap_start(c)
-            return 0
-
         lax.fori_loop(0, AHEAD, first, 0)
         for t in range(4):
             notify(barrier, (end, j, t))
@@ -196,12 +208,13 @@
             pl.semaphore_wait(ready_y, 1)
 
         a_fan(a_ref, 1, i)
-        lax.fori_loop(1, AHEAD, swap_more, 0)
+        for c in range(1, AHEAD):
+            swap_start(c)
         a_start(a_ref, 1, i, j, a_x.at[1], (z, j, x_i))
-        pltpu.make_async_copy(a_ref, a_unit(1, i, j), al_sem).start()
+        pltpu.make_async_copy(a_ref, a_unit(1, i, j), kept).start()
 
         def keep(c, _):
-            pltpu.make_async_copy(x_ref.at[c // subs, :, span(i, c % subs)], xb.at[c, i, z], xl_sem).start()
+            pltpu.make_async_copy(x_ref.at[c // subs, :, span(i, c % subs)], xb.at[c, i, z], kept).start()
             return 0
 
         lax.fori_loop(0, chunks, keep, 0)
@@ -214,8 +227,8 @@
             pass_on(c, peer, xp_recv)
             return 0
 
-        forward(0, 0)
-        lax.fori_loop(1, AHEAD, forward, 0)
+        for c in range(AHEAD):
+            forward(c, 0)
 
         def compute(c, at, size, lo=0, hi=8, done=0):
             r, sub = c // subs, c % subs
@@ -238,7 +251,7 @@
 
                 @pl.when(jnp.logical_not(mine))
                 def _():
-                    remote(yb.at[c, e, t, :, cut], o_ref.at[r, :, out], y_send, y_recv, (layer, j, t)).start()
+                    remote(yb.at[c, e, t, :, cut], o_ref.at[r, :, out], sent, y_recv, (layer, j, t)).start()
 
                 return 0
 
@@ -251,7 +264,7 @@
 
             @pl.when(s < chunks - 1)
             def _():
-                remote(xb.at[s, :, end], xb.at[s, :, end], xz_send, xp_recv.at[s], (peer, j, i)).start()
+                remote(xb.at[s, :, end], xb.at[s, :, end], sent, xp_recv.at[s], (peer, j, i)).start()
 
             @pl.when(s == last)
             def _():
@@ -296,9 +309,9 @@
             def _():
                 a_turn(1, 1)
                 a_turn(0, 1)
-                wait_bytes(a_unit(1, i, j), al_sem)
+                wait_bytes(a_unit(1, i, j), kept)
                 pl.semaphore_wait(ready, 4)
-                wait_bytes(xb.at[:, 0, 0], xl_sem)
+                wait_bytes(xb.at[:, 0, 0], kept)
                 wait_bytes(ab.at[0], a_core)
 
             @pl.when(s >= LAG)
@@ -324,12 +337,12 @@
         wait_bytes(tail_part(2), xt_recv.at[2])
         compute(last, narrow, narrow, 0, 4, 2)
         compute(last, narrow, narrow, 4, 8)
-        wait_bytes(x_ref.at[:, :, pl.ds(0, 3 * quarter)], xa_send)
-        wait_bytes(ab.at[:, pl.ds(0, 3)], a_send)
-        wait_bytes(ab.at[0, 0], a_send)
-        wait_bytes(xb.at[:, :, pl.ds(0, 2)], xz_send)
-        wait_bytes(yb.at[:, 0], y_send)
-        wait_bytes(yb.at[:, 1, pl.ds(0, 3)], y_send)
+        wait_bytes(x_ref.at[:, :, pl.ds(0, 3 * quarter)], sent)
+        wait_bytes(ab.at[:, pl.ds(0, 3)], sent)
+        wait_bytes(ab.at[0, 0], sent)
+        wait_bytes(xb.at[:, :, pl.ds(0, 2)], sent)
+        wait_bytes(yb.at[:, 0], sent)
+        wait_bytes(yb.at[:, 1, pl.ds(0, 3)], sent)
         wait_bytes(yb.at[:, 1, 0], yl_sem)
         wait_bytes(o_ref.at[:, :, pl.ds(0, 3 * quarter)], y_recv)
 
@@ -352,10 +365,10 @@
                 pltpu.VMEM((2, 4, rows, 2 * a.shape[1]), a.dtype),
                 pltpu.VMEM((chunks, 2, 4, rows, width), x.dtype),
                 pltpu.VMEM((4, rows, width // 2), jnp.float32),
-                dma, dma((4,)), dma((chunks,)), dma,
-                dma, dma((chunks,)), dma((chunks,)), dma((3,)),
-                dma, dma, dma((2,)), dma((2, 2)), dma, dma,
-                dma, dma, dma, pltpu.SemaphoreType.REGULAR, pltpu.SemaphoreType.REGULAR, pltpu.SemaphoreType.REGULAR, pltpu.SemaphoreType.REGULAR,
+                dma, dma((4,)), dma((AHEAD - 1 + (chunks - AHEAD + 1) // 2,)), dma,
+                dma((chunks,)), dma((chunks - 1,)), dma((3,)),
+                dma, dma((2,)), dma((2, 2)), dma,
+                dma, dma, pltpu.SemaphoreType.REGULAR, pltpu.SemaphoreType.REGULAR, pltpu.SemaphoreType.REGULAR, pltpu.SemaphoreType.REGULAR,
             ],
             compiler_params=pltpu.CompilerParams(collective_id=0, has_side_effects=True, vmem_limit_bytes=int(56.5 * 2**20)),
         )(x, a)

time: 214 us -> 214 us (level)
  no operation moved by 1% of the time
where the time goes in v4:
time: 214 us; the launch traced here: 213 us
  Pallas kernels  211 us (99%)
  local copies, waits for them, and re-layouts  2.19 us (1%)
    pallas_call x1, Pallas kernels, local_product(): pl.pallas_call(functools.partial(kernel, width), out_shape=pltpu.VMEM(x.s...  211 us

profile of v4, /device:TPU:0, one launch (start us, length us, event | category | flops | bytes accessed | tf_op | source)
XLA Modules:
  0.0 213.5 jit_solution(8574302984936536554)
XLA Ops:
  0.0 211.3 %shard_map.28 = bf16[3,192,4096]{2,1,0:T(8,128)(2,1)S(1)} custom-call(bf16[3,192,4096]{2,1,0:T(8,128)(2,1)} %x_ref.1, bf16[192,1536]{1,0:T(8,128)(2,1)} %a_ref.1), custom_call_target="tpu_custom_call" | custom-call | tf_op jit(solution)/shard_map/pallas_call | solution.py:358
  211.3 2.2 %copy.4 = bf16[3,192,4096]{2,1,0:T(8,128)(2,1)} copy(bf16[3,192,4096]{2,1,0:T(8,128)(2,1)S(1)} %shard_map.28) | data formatting | bytes 9437184

commit v5 on v4

--- a/solution.py
+++ b/solution.py
@@ -11,6 +11,7 @@
 WIDTH = 256
 AHEAD = 3
 LAG = 4
+BLOCKS = ((0, 3), (3, 1))
 
 
 def kernel(width, x_ref, a_ref, o_ref, xb, ab, yb, acc, sent, xa_first, xa_recv, kept, xe_recv, xp_recv, xt_recv, a_end, a_x, a_y, a_core, y_recv, yl_sem, ready_core, ready_x, ready_y, ready):
@@ -79,18 +80,13 @@
                 wait_bytes(xb.at[c, t, z], xa_first.at[t])
             remote(xb.at[c, t, z], xb.at[c, t, z], sent, arrived.at[c], (to, j, i)).start()
 
-    def tail_part(n):
-        if n == 0:
-            return xb.at[last, :, end, :, pl.ds(0, narrow)]
-        return xb.at[last, pl.ds(2 * n - 2, 2), end, :, pl.ds(narrow, narrow)]
-
     def tail_start(h):
         if h == 0:
             wait_bytes(xb.at[last, pl.ds(0, 3), z], swap_slot(last))
-        part = xb.at[last, :, z, :, pl.ds(h * narrow, narrow)]
-        remote(part, part, sent, xt_recv.at[h], (peer, j, i)).start()
-        for n in ((1, 2) if h else (0,)):
-            remote(tail_part(n), tail_part(n), sent, xt_recv.at[n], (peer, j, i)).start()
+        for n, (at, size) in enumerate(BLOCKS if h else ((0, 4),)):
+            for layer in (z, end):
+                part = xb.at[last, pl.ds(at, size), layer, :, pl.ds(h * narrow, narrow)]
+                remote(part, part, sent, xt_recv.at[n + h], (peer, j, i)).start()
 
     def a_start(src, e, row, col, arrived, where):
         remote(src, a_unit(e, row, col), sent, arrived, where).start()
@@ -330,12 +326,14 @@
             tail_start(1)
 
         compute(last, 0, narrow, 5, 8)
-        wait_bytes(xb.at[pl.ds(0, 6), 0, 0, :, pl.ds(0, narrow)], xt_recv.at[1])
-        rhs_part = xb[last, :2, :, :, pl.ds(narrow, narrow)].reshape(8 * rows, narrow)
-        lhs_part = ab[0, :, :, : 8 * rows].reshape(4 * rows, 8 * rows)
-        acc[...] = jnp.dot(lhs_part, rhs_part, preferred_element_type=jnp.float32).reshape(4, rows, narrow)
-        wait_bytes(tail_part(2), xt_recv.at[2])
-        compute(last, narrow, narrow, 0, 4, 2)
+        for n, (at, size) in enumerate(BLOCKS):
+            wait_bytes(xb.at[pl.ds(0, 2 * size), 0, 0, :, pl.ds(0, narrow)], xt_recv.at[n + 1])
+            if at + size < 4:
+                rhs_part = xb[last, at : at + size, :, :, pl.ds(narrow, narrow)].reshape(4 * size * rows, narrow)
+                lhs_part = ab[0, :, :, 4 * at * rows : 4 * (at + size) * rows].reshape(4 * rows, 4 * size * rows)
+                sums = jnp.dot(lhs_part, rhs_part, preferred_element_type=jnp.float32).reshape(4, rows, narrow)
+                acc[...] = acc[...] + sums if at else sums
+        compute(last, narrow, narrow, 0, 4, BLOCKS[-1][0])
         compute(last, narrow, narrow, 4, 8)
         wait_bytes(x_ref.at[:, :, pl.ds(0, 3 * quarter)], sent)
         wait_bytes(ab.at[:, pl.ds(0, 3)], sent)
@@ -366,7 +364,7 @@
                 pltpu.VMEM((chunks, 2, 4, rows, width), x.dtype),
                 pltpu.VMEM((4, rows, width // 2), jnp.float32),
                 dma, dma((4,)), dma((AHEAD - 1 + (chunks - AHEAD + 1) // 2,)), dma,
-                dma((chunks,)), dma((chunks - 1,)), dma((3,)),
+                dma((chunks,)), dma((chunks - 1,)), dma((1 + len(BLOCKS),)),
                 dma, dma((2,)), dma((2, 2)), dma,
                 dma, dma, pltpu.SemaphoreType.REGULAR, pltpu.SemaphoreType.REGULAR, pltpu.SemaphoreType.REGULAR, pltpu.SemaphoreType.REGULAR,
             ],

time: 214 us -> 214 us (level)
  no operation moved by 1% of the time
where the time goes in v5:
time: 214 us; the launch traced here: 213 us
  Pallas kernels  211 us (99%)
  local copies, waits for them, and re-layouts  2.19 us (1%)
    pallas_call x1, Pallas kernels, local_product(): pl.pallas_call(functools.partial(kernel, width), out_shape=pltpu.VMEM(x.s...  211 us

profile of v5, /device:TPU:0, one launch (start us, length us, event | category | flops | bytes accessed | tf_op | source)
XLA Modules:
  0.0 213.4 jit_solution(6951001007515570177)
XLA Ops:
  0.0 211.2 %shard_map.28 = bf16[3,192,4096]{2,1,0:T(8,128)(2,1)S(1)} custom-call(bf16[3,192,4096]{2,1,0:T(8,128)(2,1)} %x_ref.1, bf16[192,1536]{1,0:T(8,128)(2,1)} %a_ref.1), custom_call_target="tpu_custom_call" | custom-call | tf_op jit(solution)/shard_map/pallas_call | solution.py:356
  211.3 2.2 %copy.4 = bf16[3,192,4096]{2,1,0:T(8,128)(2,1)} copy(bf16[3,192,4096]{2,1,0:T(8,128)(2,1)S(1)} %shard_map.28) | data formatting | bytes 9437184

commit v6 on v5

--- a/solution.py
+++ b/solution.py
@@ -14,7 +14,7 @@
 BLOCKS = ((0, 3), (3, 1))
 
 
-def kernel(width, x_ref, a_ref, o_ref, xb, ab, yb, acc, sent, xa_first, xa_recv, kept, xe_recv, xp_recv, xt_recv, a_end, a_x, a_y, a_core, y_recv, yl_sem, ready_core, ready_x, ready_y, ready):
+def kernel(width, x_ref, a_ref, o_ref, xb, ab, yb, acc, sent, xa_first, xa_recv, kept, xe_recv, xp_recv, xt_recv, a_end, a_x, a_y, a_core, y_recv, ready_mid, ready):
     z = lax.axis_index("depth")
     j = lax.axis_index("col")
     i = lax.axis_index("row")
@@ -178,31 +178,22 @@
 
         @pl.when(i % 2 == 1)
         def _():
-            notify(ready_core, (z, j, core_i))
+            notify(ready_mid, (z, j, core_i))
 
         @pl.when(i >= 2)
         def _():
             for to in (x_i, other_i):
-                notify(ready_x, (z, j, to))
+                notify(ready_mid, (z, j, to))
 
         @pl.when(j == 1)
         def _():
-            notify(ready_y, (z, 0, i))
-
-        @pl.when(i % 2 == 0)
-        def _():
-            pl.semaphore_wait(ready_core, 1)
-
-        @pl.when(i < 2)
-        def _():
-            pl.semaphore_wait(ready_x, 2)
+            notify(ready_mid, (z, 0, i))
+
+        @pl.when(i + j < 4)
+        def _():
+            pl.semaphore_wait(ready_mid, 1 - i % 2 + 2 - i // 2 * 2 + 1 - j)
 
         swap_start(0)
-
-        @pl.when(j == 0)
-        def _():
-            pl.semaphore_wait(ready_y, 1)
-
         a_fan(a_ref, 1, i)
         for c in range(1, AHEAD):
             swap_start(c)
@@ -243,7 +234,7 @@
 
                 @pl.when(mine)
                 def _():
-                    pltpu.make_async_copy(yb.at[c, e, t, :, cut], o_ref.at[r, :, out], yl_sem).start()
+                    pltpu.make_async_copy(yb.at[c, e, t, :, cut], o_ref.at[r, :, out], kept).start()
 
                 @pl.when(jnp.logical_not(mine))
                 def _():
@@ -341,7 +332,7 @@
         wait_bytes(xb.at[:, :, pl.ds(0, 2)], sent)
         wait_bytes(yb.at[:, 0], sent)
         wait_bytes(yb.at[:, 1, pl.ds(0, 3)], sent)
-        wait_bytes(yb.at[:, 1, 0], yl_sem)
+        wait_bytes(yb.at[:, 1, 0], kept)
         wait_bytes(o_ref.at[:, :, pl.ds(0, 3 * quarter)], y_recv)
 
 
@@ -366,7 +357,7 @@
                 dma, dma((4,)), dma((AHEAD - 1 + (chunks - AHEAD + 1) // 2,)), dma,
                 dma((chunks,)), dma((chunks - 1,)), dma((1 + len(BLOCKS),)),
                 dma, dma((2,)), dma((2, 2)), dma,
-                dma, dma, pltpu.SemaphoreType.REGULAR, pltpu.SemaphoreType.REGULAR, pltpu.SemaphoreType.REGULAR, pltpu.SemaphoreType.REGULAR,
+                dma, pltpu.SemaphoreType.REGULAR, pltpu.SemaphoreType.REGULAR,
             ],
             compiler_params=pltpu.CompilerParams(collective_id=0, has_side_effects=True, vmem_limit_bytes=int(56.5 * 2**20)),
         )(x, a)

time: 214 us -> 214 us (level)
  no operation moved by 1% of the time
where the time goes in v6:
time: 214 us; the launch traced here: 213 us
  Pallas kernels  211 us (99%)
  local copies, waits for them, and re-layouts  2.19 us (1%)
    pallas_call x1, Pallas kernels, local_product(): pl.pallas_call(functools.partial(kernel, width), out_shape=pltpu.VMEM(x.s...  211 us

profile of v6, /device:TPU:0, one launch (start us, length us, event | category | flops | bytes accessed | tf_op | source)
XLA Modules:
  0.0 213.4 jit_solution(14208086919983736019)
XLA Ops:
  0.0 211.2 %shard_map.28 = bf16[3,192,4096]{2,1,0:T(8,128)(2,1)S(1)} custom-call(bf16[3,192,4096]{2,1,0:T(8,128)(2,1)} %x_ref.1, bf16[192,1536]{1,0:T(8,128)(2,1)} %a_ref.1), custom_call_target="tpu_custom_call" | custom-call | tf_op jit(solution)/shard_map/pallas_call | solution.py:347
  211.2 2.2 %copy.4 = bf16[3,192,4096]{2,1,0:T(8,128)(2,1)} copy(bf16[3,192,4096]{2,1,0:T(8,128)(2,1)S(1)} %shard_map.28) | data formatting | bytes 9437184

commit v7 on v6

--- a/solution.py
+++ b/solution.py
@@ -52,8 +52,8 @@
 
     def swap_start(c):
         r, sub = c // subs, c % subs
-        arrived = xa_first.at[i] if early(c) and c == 0 else swap_slot(c)
         for to in (core_i, x_i, other_i):
+            arrived = xa_first.at[(i - to + 4) % 4 - 1] if early(c) and c == 0 else swap_slot(c)
             remote(x_ref.at[r, :, span(to, sub)], xb.at[c, i, z], sent, arrived, (z, j, to)).start()
 
     def own_start(c, to, arrived):
@@ -77,7 +77,7 @@
 
         for t in (core_i, x_i, other_i):
             if early(c) and c == 0:
-                wait_bytes(xb.at[c, t, z], xa_first.at[t])
+                wait_bytes(xb.at[c, t, z], xa_first.at[(t - i + 4) % 4 - 1])
             remote(xb.at[c, t, z], xb.at[c, t, z], sent, arrived.at[c], (to, j, i)).start()
 
     def tail_start(h):
@@ -354,7 +354,7 @@
                 pltpu.VMEM((2, 4, rows, 2 * a.shape[1]), a.dtype),
                 pltpu.VMEM((chunks, 2, 4, rows, width), x.dtype),
                 pltpu.VMEM((4, rows, width // 2), jnp.float32),
-                dma, dma((4,)), dma((AHEAD - 1 + (chunks - AHEAD + 1) // 2,)), dma,
+                dma, dma((3,)), dma((AHEAD - 1 + (chunks - AHEAD + 1) // 2,)), dma,
                 dma((chunks,)), dma((chunks - 1,)), dma((1 + len(BLOCKS),)),
                 dma, dma((2,)), dma((2, 2)), dma,
                 dma, pltpu.SemaphoreType.REGULAR, pltpu.SemaphoreType.REGULAR,

time: 214 us -> 214 us (level)
  no operation moved by 1% of the time
where the time goes in v7:
time: 214 us; the launch traced here: 213 us
  Pallas kernels  211 us (99%)
  local copies, waits for them, and re-layouts  2.19 us (1%)
    pallas_call x1, Pallas kernels, local_product(): pl.pallas_call(functools.partial(kernel, width), out_shape=pltpu.VMEM(x.s...  211 us

profile of v7, /device:TPU:0, one launch (start us, length us, event | category | flops | bytes accessed | tf_op | source)
XLA Modules:
  0.0 213.4 jit_solution(49302971531312878)
XLA Ops:
  0.0 211.2 %shard_map.28 = bf16[3,192,4096]{2,1,0:T(8,128)(2,1)S(1)} custom-call(bf16[3,192,4096]{2,1,0:T(8,128)(2,1)} %x_ref.1, bf16[192,1536]{1,0:T(8,128)(2,1)} %a_ref.1), custom_call_target="tpu_custom_call" | custom-call | tf_op jit(solution)/shard_map/pallas_call | solution.py:347
  211.2 2.2 %copy.4 = bf16[3,192,4096]{2,1,0:T(8,128)(2,1)} copy(bf16[3,192,4096]{2,1,0:T(8,128)(2,1)S(1)} %shard_map.28) | data formatting | bytes 9437184
